TPU v7x, 32 devices: a whole 2x2x4 slice. The times are simulated.
32 devices in a mesh: batch: 4 (over x, y), group: 8 (over z, core).
Axes of the slice: x: 2, y: 2, z: 4, core: 2. Of those that a mesh axis runs over, the one named last changes fastest.
Arguments:
- sort_keys: float32 [262144], P(('batch', 'group')), parts along dimension 0
- seg_ids: int32 [262144], P(('batch', 'group')), parts along dimension 0
- payload: bfloat16 [262144, 768], P(('batch', 'group')), parts along dimension 0
Outputs:
- output: bfloat16 [262144, 768], P(('batch', 'group')), parts along dimension 0
There are 4 independent parts. A program takes and returns all parts, laid end to end along the dimension named above; each array names one.
All inputs are finite; a program needn't handle non-finite values.
Results may differ from a plain program's by a relative error of at most 0.00657627.
Values are sent between devices in bfloat16 or wider.
A program may use at most 1 GiB of HBM per device.

v0:
```python
import jax
import jax.numpy as jnp
from jax import lax
from jax.sharding import PartitionSpec as P


def combine_runs(left_part, right_part):
    left_flag, left_rows = left_part
    right_flag, right_rows = right_part
    joined = jnp.where(right_flag[..., None], right_rows, left_rows + right_rows)
    return jnp.logical_or(left_flag, right_flag), joined


def solution(mesh):
    group_size = mesh.shape['group']

    def per_device(sort_keys, seg_ids, payload):
        rows_dev = sort_keys.shape[0]
        width = payload.shape[1]
        pair_rows = rows_dev // group_size
        capacity = 2 * pair_rows
        my_index = lax.axis_index('group')
        local_pos = jnp.arange(rows_dev, dtype=jnp.int32)
        sorted_keys, sorted_seg, local_order = lax.sort((sort_keys, seg_ids, local_pos), num_keys=1)
        samples = sorted_keys.reshape(group_size, pair_rows)[:, 0]
        all_samples = lax.all_gather(samples, 'group', tiled=True)
        ordered_samples = jnp.sort(all_samples)
        splitters = ordered_samples.reshape(group_size, group_size)[1:, group_size // 2]
        inner_starts = jnp.searchsorted(sorted_keys, splitters, side='left').astype(jnp.int32)
        bucket_start = jnp.concatenate([jnp.zeros((1,), jnp.int32), inner_starts])
        bucket_end = jnp.concatenate([inner_starts, jnp.full((1,), rows_dev, jnp.int32)])
        slot_ids = jnp.arange(capacity, dtype=jnp.int32)
        src_index = bucket_start[:, None] + slot_ids[None, :]
        in_bucket = src_index < bucket_end[:, None]
        src_clip = jnp.minimum(src_index, rows_dev - 1)
        send_keys = jnp.where(in_bucket, sorted_keys[src_clip], jnp.inf)
        send_seg = jnp.where(in_bucket, sorted_seg[src_clip], -1)
        send_rows = jnp.where(in_bucket[..., None], payload[local_order[src_clip]], 0)
        recv_keys = lax.all_to_all(send_keys, 'group', 0, 0, tiled=True)
        recv_seg = lax.all_to_all(send_seg, 'group', 0, 0, tiled=True)
        recv_rows = lax.all_to_all(send_rows, 'group', 0, 0, tiled=True)
        flat_count = group_size * capacity
        flat_pos = jnp.arange(flat_count, dtype=jnp.int32)
        merged_keys, merged_seg, merge_order = lax.sort(
            (recv_keys.reshape(flat_count), recv_seg.reshape(flat_count), flat_pos),
            num_keys=1, is_stable=True)
        merged_rows = recv_rows.reshape(flat_count, width)[merge_order].astype(jnp.float32)
        seg_change = merged_seg[1:] != merged_seg[:-1]
        run_start = jnp.concatenate([jnp.ones((1,), dtype=jnp.bool_), seg_change])
        _, local_scan = lax.associative_scan(combine_runs, (run_start, merged_rows))
        valid_count = jnp.sum(merged_keys < jnp.inf).astype(jnp.int32)
        break_pos = jnp.min(jnp.where(seg_change, flat_pos[1:], flat_count))
        inner_break = (break_pos < valid_count).astype(jnp.int32)
        last_slot = valid_count - 1
        summary_ids = jnp.stack([merged_seg[0], merged_seg[last_slot], inner_break])
        tail_sum = local_scan[last_slot]
        all_ids = lax.all_gather(summary_ids, 'group')
        all_tails = lax.all_gather(tail_sum, 'group')
        first_all = all_ids[:, 0]
        last_all = all_ids[:, 1]
        break_all = all_ids[:, 2]
        dev_ids = jnp.arange(group_size, dtype=jnp.int32)
        link_bad = jnp.concatenate(
            [jnp.ones((1,), jnp.int32), (last_all[:-1] != first_all[1:]).astype(jnp.int32)])
        bad_links = jnp.cumsum(link_bad)
        bad_inner = jnp.cumsum(break_all)
        prev_index = jnp.maximum(my_index - 1, 0)
        carry_mask = (dev_ids < my_index) & (bad_links[my_index] == bad_links) & (bad_inner[prev_index] == bad_inner)
        carry_in = jnp.dot(carry_mask.astype(jnp.float32), all_tails, preferred_element_type=jnp.float32)
        head_run = flat_pos < break_pos
        final_rows = (local_scan + jnp.where(head_run[:, None], carry_in[None, :], 0.0)).astype(jnp.bfloat16)
        _, undo_merge = lax.sort((merge_order, flat_pos), num_keys=1)
        reply = final_rows[undo_merge].reshape(group_size, capacity, width)
        returned = lax.all_to_all(reply, 'group', 0, 0, tiled=True)
        _, sorted_rank = lax.sort((local_order, local_pos), num_keys=1)
        bucket_of = jnp.searchsorted(inner_starts, sorted_rank, side='right').astype(jnp.int32)
        slot_of = bucket_of * capacity + sorted_rank - bucket_start[bucket_of]
        return returned.reshape(flat_count, width)[slot_of]

    row_spec = P(('batch', 'group'))
    mat_spec = P(('batch', 'group'), None)
    return jax.shard_map(per_device, mesh=mesh, in_specs=(row_spec, row_spec, mat_spec),
                         out_specs=mat_spec, check_vma=False)
```

profile of v0, /device:TPU:0, one launch (start us, length us, event | category | flops | bytes accessed | tf_op | source)
XLA Modules:
  0.0 3258.6 jit_solution(3890433209734978900)
XLA Ops:
  10.2 18.1 all-reduce.28
  41.5 90.5 %gather_fusion.4 = s32[16384]{0:T(1024)S(1)} fusion(s32[8192]{0:T(1024)S(1)} %get-tuple-element.155, s32[16384]{0:T(1024)S(1)} %broadcast_clamp_fusion), kind=kCustom, calls=%fused_computation.4 | custom fusion | bytes 196608 | tf_op jit(solution)/shard_map/gather | solution.py:37
  136.2 90.5 %gather_fusion.3 = f32[16384]{0:T(1024)S(1)} fusion(f32[8192]{0:T(1024)S(1)} %get-tuple-element.389, s32[16384]{0:T(1024)S(1)} %broadcast_clamp_fusion), kind=kCustom, calls=%fused_computation.3 | custom fusion | bytes 196608 | tf_op jit(solution)/shard_map/gather | solution.py:36
  226.8 90.5 %gather_fusion.1 = s32[16384]{0:T(1024)S(1)} fusion(s32[8192]{0:T(1024)S(1)} %get-tuple-element.154, s32[16384]{0:T(1024)S(1)} %broadcast_clamp_fusion), kind=kCustom, calls=%fused_computation.1 | custom fusion | bytes 196608 | tf_op jit(solution)/shard_map/gather | solution.py:38
  318.3 79.3 %gather_fusion.2 = bf16[16384,768]{1,0:T(8,128)(2,1)} fusion(bf16[8192,768]{1,0:T(8,128)(2,1)} %param.9, s32[16384]{0:T(1024)S(1)} %broadcast_clamp_fusion.1), kind=kCustom, calls=%fused_computation.2 | custom fusion | bytes 50397184 | tf_op jit(solution)/shard_map/gather | solution.py:38
  402.6 22.2 broadcast_select_fusion.2
  466.2 508.5 %all-reduce.29 = s32[24]{0:T(128)S(1)} all-reduce(s32[24]{0:T(128)S(1)} %add_dynamic-update-slice_fusion), channel_id=3, replica_groups=mesh['batch'=4,'group'=8] {'group'}, use_global_device_ids=true, to_apply=%add.29 | all-reduce | flops 24 | bytes 192
  988.2 84.6 %gather_fusion.5 = bf16[16384,768]{1,0:T(8,128)(2,1)} fusion(bf16[16384,768]{1,0:T(8,128)(2,1)} %bitcast.2, s32[16384]{0:T(1024)S(1)} %fusion.9), kind=kCustom, calls=%fused_computation.5 | custom fusion | bytes 50397184 | tf_op jit(solution)/shard_map/gather | solution.py:47
  1074.1 110.6 %slice.369 = f32[8192,768]{1,0:T(8,128)} slice(bf16[16384,768]{1,0:T(8,128)(2,1)} %gather_fusion.5), slice={[0:16383:2], [0:768:1]} | slice | bytes 50331648 | tf_op jit(solution)/shard_map/slice | solution.py:50
  1184.8 110.6 %slice.368 = f32[8192,768]{1,0:T(8,128)} slice(bf16[16384,768]{1,0:T(8,128)(2,1)} %gather_fusion.5), slice={[1:16384:2], [0:768:1]} | slice | bytes 50331648 | tf_op jit(solution)/shard_map/slice | solution.py:50
  1295.3 112.1 %slice.366 = f32[8191,768]{1,0:T(8,128)} slice(bf16[16384,768]{1,0:T(8,128)(2,1)} %gather_fusion.5), slice={[2:16384:2], [0:768:1]} | slice | bytes 50325504 | tf_op jit(solution)/shard_map/slice | solution.py:50
  1407.4 16.4 add_select_fusion.1
  1432.2 57.1 %slice.376 = f32[4096,768]{1,0:T(8,128)} slice(f32[8192,768]{1,0:T(8,128)} %copy-done.2), slice={[0:8191:2], [0:768:1]} | slice | bytes 25165824 | tf_op jit(solution)/shard_map/slice | solution.py:50
  1489.3 57.1 %slice.375 = f32[4096,768]{1,0:T(8,128)} slice(f32[8192,768]{1,0:T(8,128)} %copy-done.2), slice={[1:8192:2], [0:768:1]} | slice | bytes 25165824 | tf_op jit(solution)/shard_map/slice | solution.py:50
  1546.4 57.6 %slice.373 = f32[4095,768]{1,0:T(8,128)} slice(f32[8192,768]{1,0:T(8,128)} %copy-done.2), slice={[2:8192:2], [0:768:1]} | slice | bytes 25159680 | tf_op jit(solution)/shard_map/slice | solution.py:50
  1618.0 29.2 slice.383
  1647.2 29.2 slice.382
  1676.4 29.4 slice.380
  1862.5 18.7 pad.106
  1897.6 36.2 %pad.107 = f32[4096,768]{1,0:T(8,128)} pad(f32[2048,768]{1,0:T(8,128)} %pad_maximum_fusion.2, f32[]{:T(128)} %constant.158.clone.1), padding=0_1_1x0_0_0 | pad | bytes 18874372 | tf_op jit(solution)/shard_map/pad | solution.py:50
  1933.8 36.5 %pad.108 = f32[4096,768]{1,0:T(8,128)} pad(f32[2048,768]{1,0:T(8,128)} %add.353, f32[]{:T(128)} %constant.158.clone.1), padding=1_0_1x0_0_0 | pad | bytes 18874372 | tf_op jit(solution)/shard_map/pad | solution.py:50
  2011.1 72.1 %pad.109 = f32[8192,768]{1,0:T(8,128)} pad(f32[4096,768]{1,0:T(8,128)} %pad_maximum_fusion.1, f32[]{:T(128)} %constant.158.clone.1), padding=0_1_1x0_0_0 | pad | bytes 37748740 | tf_op jit(solution)/shard_map/pad | solution.py:50
  2083.2 72.2 %pad.110 = f32[8192,768]{1,0:T(8,128)} pad(f32[4096,768]{1,0:T(8,128)} %add.355, f32[]{:T(128)} %constant.158.clone.1), padding=1_0_1x0_0_0 | pad | bytes 37748740 | tf_op jit(solution)/shard_map/pad | solution.py:50
  2155.4 25.9 add.357
  2181.3 33.0 %add_select_fusion = f32[8191,768]{1,0:T(8,128)} fusion(f32[8191,768]{1,0:T(8,128)} %slice.366, f32[8192,768]{1,0:T(8,128)} %pad.110, f32[8192,768]{1,0:T(8,128)} %pad.109, pred[8191]{0:T(1024)(128)(4,1)S(1)} %copy-done.15), kind=kLoop, calls=%fused_computation.27 | loop fusion | flops 18872064 | bytes 100659200 | tf_op jit(solution)/shard_map/jit(_where)/select_n | solution.py:10
  2214.3 17.1 pad_maximum_fusion
  2231.4 143.7 %pad.111 = f32[16384,768]{1,0:T(8,128)} pad(f32[8192,768]{1,0:T(8,128)} %pad_maximum_fusion, f32[]{:T(128)} %constant.158.clone.1), padding=0_1_1x0_0_0 | pad | bytes 75497472 | tf_op jit(solution)/shard_map/pad | solution.py:50
  2375.1 143.9 %pad.112 = f32[16384,768]{1,0:T(8,128)} pad(f32[8192,768]{1,0:T(8,128)} %add.357, f32[]{:T(128)} %constant.158.clone.1), padding=1_0_1x0_0_0 | pad | bytes 75497472 | tf_op jit(solution)/shard_map/pad | solution.py:50
  2534.5 40.7 %add_convert_fusion = bf16[16384,768]{1,0:T(8,128)(2,1)} fusion(f32[16384,768]{1,0:T(8,128)} %pad.111, f32[16384,768]{1,0:T(8,128)} %pad.112, f32[768]{0:T(1024)S(1)} %convolution_reduce_fusion, pred[16384]{0:T(1024)(128)(4,1)S(1)} %copy-done.14), kind=kLoop, calls=%fused_computation.26 | loop fusion | flops 50331648 | bytes 125848576 | tf_op jit(solution)/shard_map/convert_element_type | solution.py:71
  2575.1 84.5 %gather_fusion.6 = bf16[16384,768]{1,0:T(8,128)(2,1)} fusion(bf16[16384,768]{1,0:T(8,128)(2,1)} %add_convert_fusion, s32[16384]{0:T(1024)S(1)} %copy-done.13), kind=kCustom, calls=%fused_computation.6 | custom fusion | bytes 50397184 | tf_op jit(solution)/shard_map/gather | solution.py:73
  2692.8 516.9 %all-to-all-done.3 = bf16[8,2048,768]{2,1,0:T(8,128)(2,1)} async-done(((bf16[8,2048,768]{2,1,0:T(8,128)(2,1)}), bf16[8,2048,768]{2,1,0:T(8,128)(2,1)}, u32[]{:S(2)}, u32[]{:S(2)}) %all-to-all-start.3) | async-done | bytes 25165856 | tf_op jit(solution)/shard_map/all_to_all | solution.py:74
  3209.7 48.4 %gather_fusion.7 = bf16[8192,768]{1,0:T(8,128)(2,1)} fusion(bf16[16384,768]{1,0:T(8,128)(2,1)} %bitcast.18, s32[8192]{0:T(1024)S(1)} %fusion.12), kind=kCustom, calls=%fused_computation.7 | custom fusion | bytes 25198592 | tf_op jit(solution)/shard_map/gather | solution.py:78
  (411 shorter events, 393.7 us)
Async XLA Ops:
  8.0 218.8 %copy-start = (s32[8192]{0:T(1024)}, s32[8192]{0:T(1024)S(1)}, u32[]{:S(2)}) copy-start(s32[8192]{0:T(1024)S(1)} %get-tuple-element.154) | copy-start | bytes 98308
  132.9 264.7 %all-to-all-start.2 = ((s32[8,1,2048]{2,1,0:T(1,128)}), s32[8,1,2048]{2,1,0:T(1,128)S(1)}, u32[]{:S(2)}, u32[]{:S(2)}) async-start(s32[8,1,2048]{2,1,0:T(1,128)} %compare_select_fusion.9), calls=%async_computation.2 | async-start | bytes 131072 | tf_op jit(solution)/shard_map/all_to_all | solution.py:40
  397.6 27.2 all-to-all-start.1
  424.8 563.4 %all-to-all-start = ((bf16[8,2048,768]{2,1,0:T(8,128)(2,1)}), bf16[8,2048,768]{2,1,0:T(8,128)(2,1)}, u32[]{:S(2)}, u32[]{:S(2)}) async-start(bf16[8,2048,768]{2,1,0:T(8,128)(2,1)} %broadcast_select_fusion.2), calls=%async_computation | async-start | bytes 50331648 | tf_op jit(solution)/shard_map/all_to_all | solution.py:41
  449.2 623.6 %copy-start.16 = (pred[2048]{0:T(1024)(128)(4,1)}, pred[2048]{0:T(1024)(128)(4,1)S(1)}, u32[]{:S(2)}) copy-start(pred[2048]{0:T(1024)(128)(4,1)S(1)} %slice.381) | copy-start | bytes 6148
  450.7 524.0 %copy-start.20 = (pred[1024]{0:T(1024)(128)(4,1)}, pred[1024]{0:T(1024)(128)(4,1)S(1)}, u32[]{:S(2)}) copy-start(pred[1024]{0:T(1024)(128)(4,1)S(1)} %slice.388) | copy-start | bytes 3076
  452.0 525.2 %copy-start.34 = (pred[512]{0:T(512)(128)(4,1)}, pred[512]{0:T(512)(128)(4,1)S(1)}, u32[]{:S(2)}) copy-start(pred[512]{0:T(512)(128)(4,1)S(1)} %slice.395) | copy-start | bytes 1540
  459.2 515.5 %copy-start.26 = (pred[4]{0:T(512)(128)(4,1)}, pred[4]{0:T(512)(128)(4,1)S(1)}, u32[]{:S(2)}) copy-start(pred[4]{0:T(512)(128)(4,1)S(1)} %slice.444) | copy-start | bytes 16
  460.6 516.6 %copy-start.37 = (pred[2]{0:T(512)(128)(4,1)}, pred[2]{0:T(512)(128)(4,1)S(1)}, u32[]{:S(2)}) copy-start(pred[2]{0:T(512)(128)(4,1)S(1)} %slice.451) | copy-start | bytes 10
  975.3 97.5 %copy-start.39 = (s32[8,1]{0,1:T(1,128)}, s32[8,1]{0,1:T(1,128)S(1)}, u32[]{:S(2)}) copy-start(s32[8,1]{0,1:T(1,128)S(1)} %reduce-window.6) | copy-start | bytes 100
  1647.2 58.7 %copy-start.17 = (pred[2048]{0:T(1024)(128)(4,1)S(1)}, pred[2048]{0:T(1024)(128)(4,1)}, u32[]{:S(2)}) copy-start(pred[2048]{0:T(1024)(128)(4,1)} %copy-done.16) | copy-start | bytes 6148
  1713.5 45.6 %copy-start.21 = (pred[1024]{0:T(1024)(128)(4,1)S(1)}, pred[1024]{0:T(1024)(128)(4,1)}, u32[]{:S(2)}) copy-start(pred[1024]{0:T(1024)(128)(4,1)} %copy-done.20) | copy-start | bytes 3076
  1743.9 33.7 %copy-start.35 = (pred[512]{0:T(512)(128)(4,1)S(1)}, pred[512]{0:T(512)(128)(4,1)}, u32[]{:S(2)}) copy-start(pred[512]{0:T(512)(128)(4,1)} %copy-done.34) | copy-start | bytes 1540
  1759.1 36.1 %copy-start.33 = (pred[256]{0:T(512)(128)(4,1)S(1)}, pred[256]{0:T(512)(128)(4,1)}, u32[]{:S(2)}) copy-start(pred[256]{0:T(512)(128)(4,1)} %copy-done.32) | copy-start | bytes 772
  1762.4 46.6 %copy-start.7 = (f32[1024,768]{1,0:T(8,128)}, f32[1024,768]{1,0:T(8,128)S(1)}, u32[]{:S(2)}) copy-start(f32[1024,768]{1,0:T(8,128)S(1)} %add_select_fusion.7) | copy-start | bytes 9437188
  1762.4 44.6 %copy-start.31 = (pred[128]{0:T(512)(128)(4,1)S(1)}, pred[128]{0:T(512)(128)(4,1)}, u32[]{:S(2)}) copy-start(pred[128]{0:T(512)(128)(4,1)} %copy-done.30) | copy-start | bytes 388
  1772.6 46.0 %copy-start.25 = (pred[31]{0:T(512)(128)(4,1)S(1)}, pred[31]{0:T(512)(128)(4,1)}, u32[]{:S(2)}) copy-start(pred[31]{0:T(512)(128)(4,1)} %slice.421) | copy-start | bytes 97
  1797.7 25.2 slice-start.6
  1797.7 23.1 slice-start.7
  1828.7 19.6 copy-start.23
  1834.6 17.1 slice-start.4
  1862.5 27.5 slice-start.2
  1862.5 27.5 copy-start.22
  1970.3 16.4 copy-start.3
  1970.3 16.4 copy-start.18
  2155.4 25.9 copy-start.15
  2181.3 33.0 %copy-start.19 = (f32[1,768]{1,0:T(1,128)S(1)}, f32[1,768]{1,0:T(1,128)}, u32[]{:S(2)}) copy-start(f32[1,768]{1,0:T(1,128)} %slice.524) | copy-start | bytes 9220
  2375.1 158.5 %copy-start.36 = (pred[8]{0:T(512)(128)(4,1)S(1)}, pred[8]{0:T(512)(128)(4,1)}, u32[]{:S(2)}) copy-start(pred[8]{0:T(512)(128)(4,1)} %compare_reduce_fusion) | copy-start | bytes 28
  2375.1 158.5 %copy-start.40 = (s32[8,1]{0,1:T(1,128)S(1)}, s32[8,1]{0,1:T(1,128)}, u32[]{:S(2)}) copy-start(s32[8,1]{0,1:T(1,128)} %copy-done.39) | copy-start | bytes 100
  2375.1 159.4 %copy-start.14 = (pred[16384]{0:T(1024)(128)(4,1)S(1)}, pred[16384]{0:T(1024)(128)(4,1)}, u32[]{:S(2)}) copy-start(pred[16384]{0:T(1024)(128)(4,1)} %iota_compare_fusion) | copy-start | bytes 49156
  2534.5 40.7 %copy-start.13 = (s32[16384]{0:T(1024)S(1)}, s32[16384]{0:T(1024)}, u32[]{:S(2)}) copy-start(s32[16384]{0:T(1024)} %fusion.10) | copy-start | bytes 196612
  2659.6 550.0 %all-to-all-start.3 = ((bf16[8,2048,768]{2,1,0:T(8,128)(2,1)}), bf16[8,2048,768]{2,1,0:T(8,128)(2,1)}, u32[]{:S(2)}, u32[]{:S(2)}) async-start(bf16[8,2048,768]{2,1,0:T(8,128)(2,1)} %bitcast.68), calls=%async_computation.3 | async-start | bytes 50331648 | tf_op jit(solution)/shard_map/all_to_all | solution.py:74
  (21 other events, 113.7 us)
where the time goes:
time: 3300 us; the launch traced here: 3260 us
  local copies, waits for them, and re-layouts  1860 us (56%)
  blocking collectives  541 us (16%)
  waiting for transfers between devices  517 us (16%)
  other arithmetic  315 us (10%)
    slice x96, local copies, waits for them, and re-layouts, per_device(): _, local_scan = lax.associative_scan(combine_runs, (run_start, merged_rows))  701 us
    pad x26, local copies, waits for them, and re-layouts, per_device(): _, local_scan = lax.associative_scan(combine_runs, (run_start, merged_rows))  551 us
    all_to_all x1, waiting for transfers between devices, per_device(): returned = lax.all_to_all(reply, 'group', 0, 0, tiled=True)  517 us
    unnamed x1, blocking collectives  509 us
    select_n x25, other arithmetic, combine_runs(): jnp.where(right_flag[..., None], right_rows, left_rows + right_rows)  104 us
    gather x2, local copies, waits for them, and re-layouts, per_device(): local_order[src_clip]  90.6 us
    gather x1, local copies, waits for them, and re-layouts, per_device(): send_seg = jnp.where(in_bucket, sorted_seg[src_clip], -1)  90.5 us
    gather x1, local copies, waits for them, and re-layouts, per_device(): send_keys = jnp.where(in_bucket, sorted_keys[src_clip], jnp.inf)  90.5 us
  transfers between devices with their start and end apart: 4, of which 1 were waited for; matrix products, arithmetic and copies ran while one was open for 11% of the time, Pallas kernels for 0%

commit v1 on v0

v1 whole, which is shorter than its diff:
```python
import functools

import jax
import jax.numpy as jnp
from jax import lax
from jax.experimental import pallas as pl
from jax.experimental.pallas import tpu as pltpu
from jax.sharding import PartitionSpec as P

LANES = 128
BLOCKS = 4
WIDE = LANES // BLOCKS
ROWS_STEP = 32
SUB = 8
SPAN = 128


def lane_block(shape):
    return lax.broadcasted_iota(jnp.int32, shape, 1) // WIDE


def swap_blocks(parts):
    block = lane_block(parts[0].shape)
    odd = (block % 2) == 1
    high = block >= 2
    one = []
    for k in range(0, BLOCKS, 2):
        a, b = parts[k], parts[k + 1]
        one.append(jnp.where(odd, pltpu.roll(b, WIDE, 1), a))
        one.append(jnp.where(odd, b, pltpu.roll(a, LANES - WIDE, 1)))
    out = [None] * BLOCKS
    for k in range(2):
        a, b = one[k], one[k + 2]
        out[k] = jnp.where(high, pltpu.roll(b, 2 * WIDE, 1), a)
        out[k + 2] = jnp.where(high, b, pltpu.roll(a, 2 * WIDE, 1))
    return out


def pack_kernel(src, dst):
    step_rows = src.shape[1]

    def step(k, carry):
        rows = pl.ds(pl.multiple_of(k * ROWS_STEP, ROWS_STEP), ROWS_STEP)
        for t in range(2):
            cols = slice(t * LANES, (t + 1) * LANES)
            parts = [src[q, rows, cols].astype(jnp.float32) for q in range(BLOCKS)]
            for l, part in enumerate(swap_blocks(parts)):
                dst[t * BLOCKS + l, rows, :] = part.astype(jnp.bfloat16)
        return carry

    lax.fori_loop(0, step_rows // ROWS_STEP, step, 0)


def unpack_kernel(src, *refs):
    dst = refs[-1]
    step_rows = src.shape[1]

    def step(k, carry):
        rows = pl.ds(pl.multiple_of(k * ROWS_STEP, ROWS_STEP), ROWS_STEP)
        for t in range(2):
            cols = slice(t * LANES, (t + 1) * LANES)
            parts = [src[t * BLOCKS + l, rows, :].astype(jnp.float32) for l in range(BLOCKS)]
            for q, part in enumerate(swap_blocks(parts)):
                dst[q, rows, cols] = part.astype(jnp.bfloat16)
        return carry

    lax.fori_loop(0, step_rows // ROWS_STEP, step, 0)


def walk_kernel(group_size, order, starts, spans, src, dst, grid_rows):
    packed_rows = src.shape[0]
    quarter = grid_rows.shape[0] // (group_size * BLOCKS)
    per_dev = quarter

    def spread(k, carry):
        base = pl.multiple_of(k * ROWS_STEP, ROWS_STEP)
        dev = base // per_dev
        row = base % per_dev
        data = src[pl.ds(base, ROWS_STEP), :].astype(jnp.float32)
        for q in range(BLOCKS):
            at = pl.multiple_of((dev * BLOCKS + q) * quarter + row, ROWS_STEP)
            moved = data if q == 0 else pltpu.roll(data, LANES - q * WIDE, 1)
            grid_rows[pl.ds(at, ROWS_STEP), :] = moved
        return carry

    lax.fori_loop(0, packed_rows // ROWS_STEP, spread, 0)

    def load(base):
        index = [order[base + u] for u in range(SUB)]
        return index, [grid_rows[pl.ds(i, 1), :] for i in index]

    def plain(n, total):
        base = n * SPAN
        index, rows = load(base)
        for k in range(SPAN // SUB):
            now_index, now_rows = index, rows
            if k + 1 < SPAN // SUB:
                index, rows = load(base + (k + 1) * SUB)
            for g in range(0, SUB, 4):
                a, b, c, d = now_rows[g:g + 4]
                ab = a + b
                abc = ab + c
                abcd = ab + (c + d)
                sums = (total + a, total + ab, total + abc, total + abcd)
                total = sums[3]
                for u in range(4):
                    grid_rows[pl.ds(now_index[g + u], 1), :] = sums[u]
        return total

    def broken(n, total):
        def one(u, total):
            t = n * SPAN + u
            row = pl.ds(order[t], 1)
            new = starts[t // 16]
            fresh = ((new >> (t % 16)) & 1) == 1
            value = grid_rows[row, :]
            total = jnp.where(fresh, value, total + value)
            grid_rows[row, :] = total
            return total

        return lax.fori_loop(0, SPAN, one, total)

    def walk(n, total):
        return lax.cond(spans[0, n] == 0, plain, broken, n, total)

    lax.fori_loop(0, spans.shape[1], walk, jnp.zeros((1, LANES), jnp.float32))

    block = lane_block((ROWS_STEP, LANES))

    def gather(k, carry):
        base = pl.multiple_of(k * ROWS_STEP, ROWS_STEP)
        dev = base // per_dev
        row = base % per_dev
        merged = None
        for q in range(BLOCKS):
            at = pl.multiple_of((dev * BLOCKS + q) * quarter + row, ROWS_STEP)
            data = grid_rows[pl.ds(at, ROWS_STEP), :]
            merged = data if q == 0 else jnp.where(block == q, pltpu.roll(data, q * WIDE, 1), merged)
        dst[pl.ds(base, ROWS_STEP), :] = merged.astype(jnp.bfloat16)
        return carry

    lax.fori_loop(0, packed_rows // ROWS_STEP, gather, 0)


def solution(mesh):
    group_size = mesh.shape['group']

    def per_device(sort_keys, seg_ids, payload):
        rows_dev = sort_keys.shape[0]
        width = payload.shape[1]
        quarter = rows_dev // BLOCKS
        count = group_size * rows_dev
        chunk_cols = group_size * WIDE
        chunks = width // chunk_cols
        tile = min(512, quarter)

        def pack(c, folded):
            return pl.pallas_call(
                pack_kernel, name=f'pack{c}',
                out_shape=jax.ShapeDtypeStruct((group_size, quarter, LANES), jnp.bfloat16),
                grid=(quarter // tile,),
                in_specs=[pl.BlockSpec((BLOCKS, tile, chunk_cols), lambda i: (0, i, c))],
                out_specs=pl.BlockSpec((group_size, tile, LANES), lambda i: (0, i, 0)),
                compiler_params=pltpu.CompilerParams(vmem_limit_bytes=60 * 2**20),
                cost_estimate=pl.CostEstimate(flops=50_000_000, bytes_accessed=2 * rows_dev * chunk_cols * 2,
                                              transcendentals=0),
            )(folded)

        def unpack(c, back, out):
            first = out is None
            return pl.pallas_call(
                unpack_kernel, name=f'unpack{c}',
                out_shape=jax.ShapeDtypeStruct((BLOCKS, quarter, width), jnp.bfloat16),
                grid=(quarter // tile,),
                in_specs=[pl.BlockSpec((group_size, tile, LANES), lambda i: (0, i, 0))]
                + ([] if first else [pl.BlockSpec(memory_space=pl.ANY)]),
                out_specs=pl.BlockSpec((BLOCKS, tile, chunk_cols), lambda i: (0, i, c)),
                input_output_aliases={} if first else {1: 0},
                compiler_params=pltpu.CompilerParams(vmem_limit_bytes=60 * 2**20),
                cost_estimate=pl.CostEstimate(flops=50_000_000, bytes_accessed=2 * rows_dev * chunk_cols * 2,
                                              transcendentals=0),
            )(*((back,) if first else (back, out)))

        def walk(c, order, starts, spans, rows):
            return pl.pallas_call(
                functools.partial(walk_kernel, group_size), name=f'walk{c}',
                out_shape=jax.ShapeDtypeStruct((count // BLOCKS, LANES), jnp.bfloat16),
                in_specs=[pl.BlockSpec(memory_space=pltpu.SMEM)] * 3 + [pl.BlockSpec(memory_space=pltpu.VMEM)],
                out_specs=pl.BlockSpec(memory_space=pltpu.VMEM),
                scratch_shapes=[pltpu.VMEM((count, LANES), jnp.float32)],
                compiler_params=pltpu.CompilerParams(vmem_limit_bytes=60 * 2**20),
                cost_estimate=pl.CostEstimate(flops=1_000_000_000, bytes_accessed=2 * count * WIDE * 2,
                                              transcendentals=0),
            )(order, starts, spans, rows)

        halves = jnp.stack([sort_keys, (seg_ids >> 16).astype(jnp.float32), (seg_ids & 0xFFFF).astype(jnp.float32)])
        every = lax.all_gather(halves, 'group')
        every, folded = lax.optimization_barrier((every, payload.reshape(BLOCKS, quarter, width)))
        keys = every[:, 0].reshape(count)
        ids = ((every[:, 1].astype(jnp.int32) << 16) | every[:, 2].astype(jnp.int32)).reshape(count)
        first = pack(0, folded)
        _, ids_sorted, order = lax.sort((keys, ids, jnp.arange(count, dtype=jnp.int32)), num_keys=1)
        new = jnp.concatenate([jnp.ones((1,), jnp.bool_), ids_sorted[1:] != ids_sorted[:-1]]).astype(jnp.int32)
        starts = jnp.sum(new.reshape(count // 16, 16) << jnp.arange(16, dtype=jnp.int32)[None, :], axis=1)
        spans = jnp.max(new.reshape(1, count // SPAN, SPAN), axis=2)
        order, starts, spans, folded = lax.optimization_barrier((order, starts, spans, folded))

        sent = [first] + [pack(c, folded) for c in range(1, chunks)]
        there = [lax.all_to_all(s, 'group', 0, 0, tiled=True) for s in sent]
        done = [walk(c, order, starts, spans, there[c].reshape(count // BLOCKS, LANES)) for c in range(chunks)]
        back = [lax.all_to_all(d.reshape(group_size, quarter, LANES), 'group', 0, 0, tiled=True) for d in done]
        out = None
        for c in range(chunks):
            out = unpack(c, back[c], out)
        return out.reshape(rows_dev, width)

    row_spec = P(('batch', 'group'))
    mat_spec = P(('batch', 'group'), None)
    return jax.shard_map(per_device, mesh=mesh, in_specs=(row_spec, row_spec, mat_spec),
                         out_specs=mat_spec, check_vma=False)
```

time: 3300 us -> 935 us (0.28); the launches traced: 3260 us -> 934 us
  local copies, waits for them, and re-layouts: 1860 us -> 0.8 us
  Pallas kernels: 0 us -> 654 us
  blocking collectives: 541 us -> 18.4 us
  waiting for transfers between devices: 517 us -> 173 us
  other arithmetic: 315 us -> 58.1 us
    slice x100 -> x1, local copies, waits for them, and re-layouts: 702 us -> 0.18 us  [per_device(): keys = every[:, 0].reshape(count)]
    pallas_call x0 -> x9, Pallas kernels: none -> 654 us  [the longest x3 578 us: walk(): pl.pallas_call(functools.partial(walk_kernel, group_size), name=f'walk{c}...]
    gather x26 -> x0, local copies, waits for them, and re-layouts: 580 us -> none  [the longest x2 90.6 us: per_device(): local_order[src_clip]]
    pad x26 -> x0, local copies, waits for them, and re-layouts: 551 us -> none  [per_device(): _, local_scan = lax.associative_scan(combine_runs, (run_start, merged_rows))]
    unnamed x1 -> x0, blocking collectives: 509 us -> none
    all_to_all x4 -> x6, waiting for transfers between devices: 517 us -> 173 us  [the longest x3 105 us: per_device(): there = [lax.all_to_all(s, 'group', 0, 0, tiled=True) for s in sent]]
    select_n x59 -> x0, other arithmetic: 141 us -> none  [the longest x25 104 us: combine_runs(): jnp.where(right_flag[..., None], right_rows, left_rows + right_rows)]
    add x27 -> x0, other arithmetic: 55.7 us -> none  [the longest x13 55.6 us: per_device(): _, local_scan = lax.associative_scan(combine_runs, (run_start, merged_rows))]
  transfers between devices with their start and end apart: 4 -> 6, of which waited for: 1 -> 3; matrix products, arithmetic and copies ran while one was open for 11% -> 6% of each run, Pallas kernels for 0% -> 67%
where the time goes in v1:
time: 935 us; the launch traced here: 934 us
  Pallas kernels  654 us (70%)
  waiting for transfers between devices  173 us (19%)
  other arithmetic  58.1 us (6%)
  starting transfers between devices  29.5 us (3%)
  blocking collectives  18.4 us (2%)
    pallas_call x3, Pallas kernels, walk(): pl.pallas_call(functools.partial(walk_kernel, group_size), name=f'walk{c}...  578 us
    all_to_all x3, waiting for transfers between devices, per_device(): there = [lax.all_to_all(s, 'group', 0, 0, tiled=True) for s in sent]  105 us
    all_to_all x3, waiting for transfers between devices, per_device(): lax.all_to_all(d.reshape(group_size, quarter, LANES), 'group', 0, 0, tile...  68.4 us
    sort x1, other arithmetic, per_device(): lax.sort((keys, ids, jnp.arange(count, dtype=jnp.int32)), num_keys=1)  53.5 us
    pallas_call x3, Pallas kernels, pack(): pl.pallas_call(pack_kernel, name=f'pack{c}', out_shape=jax.ShapeDtypeStru...  38.2 us
    pallas_call x3, Pallas kernels, unpack(): pl.pallas_call(unpack_kernel, name=f'unpack{c}', out_shape=jax.ShapeDtype...  38.1 us
  transfers between devices with their start and end apart: 6, of which 3 were waited for; matrix products, arithmetic and copies ran while one was open for 6% of the time, Pallas kernels for 67%

profile of v1, /device:TPU:0, one launch (start us, length us, event | category | flops | bytes accessed | tf_op | source)
XLA Modules:
  0.0 934.3 jit_solution(12278544954357617077)
XLA Ops:
  0.0 0.8 shift-right-arithmetic_convert_fusion
  0.8 0.8 maximum_bitcast_fusion
  1.6 18.4 %all-gather.1 = f32[8,3,8192]{2,1,0:T(4,128)S(1)} all-gather(f32[1,3,8192]{2,1,0:T(4,128)S(1)} %maximum_bitcast_fusion), channel_id=2, replica_groups=mesh['batch'=4,'group'=8] {'group'}, dimensions={0}, use_global_device_ids=true | all-gather | bytes 884736 | tf_op jit(solution)/shard_map/all_gather | solution.py:197
  20.0 12.7 %pack0.1 = bf16[8,2048,128]{2,1,0:T(8,128)(2,1)} custom-call(bf16[4,2048,768]{2,1,0:T(8,128)(2,1)} %bitcast.18), custom_call_target="tpu_custom_call" | custom-call | flops 50000000 | bytes 8388608 | tf_op jit(solution)/shard_map/pack0/pallas_call | solution.py:158
  32.7 5.2 all-to-all-start.4
  37.9 0.2 slice.15
  38.1 0.7 convert_or_fusion
  38.8 53.5 %sort.21 = (f32[65536]{0:T(1024)}, s32[65536]{0:T(1024)S(1)}, s32[65536]{0:T(1024)}) sort(f32[65536]{0:T(1024)S(1)} %bitcast.25, s32[65536]{0:T(1024)S(1)} %bitcast.24, s32[65536]{0:T(1024)S(1)} %iota.7), dimensions={0}, to_apply=%region_0.0 | sort | flops 1048576 | bytes 1572864 | tf_op jit(solution)/shard_map/sort | solution.py:202
  92.3 0.1 slice_compare_fusion
  92.4 0.1 add_convert_fusion
  92.6 0.6 reshape.59
  93.2 0.8 bitcast_reduce_fusion
  94.0 1.2 shift-left_reduce_fusion.starts
  95.2 12.8 %pack1.1 = bf16[8,2048,128]{2,1,0:T(8,128)(2,1)} custom-call(bf16[4,2048,768]{2,1,0:T(8,128)(2,1)} %bitcast.19), custom_call_target="tpu_custom_call" | custom-call | flops 50000000 | bytes 8388608 | tf_op jit(solution)/shard_map/pack1/pallas_call | solution.py:158
  108.0 23.7 %all-to-all-done.4 = bf16[8,2048,128]{2,1,0:T(8,128)(2,1)} async-done(((bf16[8,2048,128]{2,1,0:T(8,128)(2,1)}), bf16[8,2048,128]{2,1,0:T(8,128)(2,1)}, u32[]{:S(2)}, u32[]{:S(2)}) %all-to-all-start.4) | async-done | bytes 4194336 | tf_op jit(solution)/shard_map/all_to_all | solution.py:209
  131.7 4.6 all-to-all-start.2
  136.3 12.7 %pack2.1 = bf16[8,2048,128]{2,1,0:T(8,128)(2,1)} custom-call(bf16[4,2048,768]{2,1,0:T(8,128)(2,1)} %bitcast.20), custom_call_target="tpu_custom_call" | custom-call | flops 50000000 | bytes 8388608 | tf_op jit(solution)/shard_map/pack2/pallas_call | solution.py:158
  149.0 80.9 %all-to-all-done.2 = bf16[8,2048,128]{2,1,0:T(8,128)(2,1)} async-done(((bf16[8,2048,128]{2,1,0:T(8,128)(2,1)}), bf16[8,2048,128]{2,1,0:T(8,128)(2,1)}, u32[]{:S(2)}, u32[]{:S(2)}) %all-to-all-start.2) | async-done | bytes 4194336 | tf_op jit(solution)/shard_map/all_to_all | solution.py:209
  229.9 4.5 all-to-all-start
  234.5 192.7 %walk0.1 = bf16[16384,128]{1,0:T(8,128)(2,1)} custom-call(s32[65536]{0:T(1024)} %get-tuple-element.17.order, s32[4096]{0:T(1024)} %shift-left_reduce_fusion.starts, s32[1,512]{1,0:T(1,128)} %bitcast.28, bf16[16384,128]{1,0:T(8,128)(2,1)} %bitcast.13.src), custom_call_target="tpu_custom_call" | custom-call | flops 1000000000 | bytes 8388608 | tf_op jit(solution)/shard_map/walk0/pallas_call | solution.py:185
  427.2 0.0 all-to-all-done
  427.2 5.0 all-to-all-start.5
  432.2 192.7 %walk1.1 = bf16[16384,128]{1,0:T(8,128)(2,1)} custom-call(s32[65536]{0:T(1024)} %get-tuple-element.17.order, s32[4096]{0:T(1024)} %shift-left_reduce_fusion.starts, s32[1,512]{1,0:T(1,128)} %bitcast.29, bf16[16384,128]{1,0:T(8,128)(2,1)} %bitcast.11.src), custom_call_target="tpu_custom_call" | custom-call | flops 1000000000 | bytes 8388608 | tf_op jit(solution)/shard_map/walk1/pallas_call | solution.py:185
  624.9 0.0 all-to-all-done.5.src
  624.9 5.1 all-to-all-start.3
  630.0 192.7 %walk2.1 = bf16[16384,128]{1,0:T(8,128)(2,1)} custom-call(s32[65536]{0:T(1024)} %get-tuple-element.17.order, s32[4096]{0:T(1024)} %shift-left_reduce_fusion.starts, s32[1,512]{1,0:T(1,128)} %bitcast.30, bf16[16384,128]{1,0:T(8,128)(2,1)} %bitcast.9.src), custom_call_target="tpu_custom_call" | custom-call | flops 1000000000 | bytes 8388608 | tf_op jit(solution)/shard_map/walk2/pallas_call | solution.py:185
  822.7 0.0 all-to-all-done.3.src
  822.7 5.1 all-to-all-start.1
  827.8 12.7 %unpack0.1.refs_0_ = bf16[4,2048,768]{2,1,0:T(8,128)(2,1)} custom-call(bf16[8,2048,128]{2,1,0:T(8,128)(2,1)} %all-to-all-done.5.src), custom_call_target="tpu_custom_call" | custom-call | flops 50000000 | bytes 8388608 | tf_op jit(solution)/shard_map/unpack0/pallas_call | solution.py:171
  840.5 12.7 %unpack1.1.refs_0_ = bf16[4,2048,768]{2,1,0:T(8,128)(2,1)} custom-call(bf16[8,2048,128]{2,1,0:T(8,128)(2,1)} %all-to-all-done.3.src, bf16[4,2048,768]{2,1,0:T(8,128)(2,1)} %unpack0.1.refs_0_), custom_call_target="tpu_custom_call", output_to_operand_aliasing={{}: (1, {})} | custom-call | flops 50000000 | bytes 8388608 | tf_op jit(solution)/shard_map/unpack1/pallas_call | solution.py:171
  853.2 68.4 %all-to-all-done.1.src = bf16[8,2048,128]{2,1,0:T(8,128)(2,1)} async-done(((bf16[8,2048,128]{2,1,0:T(8,128)(2,1)}), bf16[8,2048,128]{2,1,0:T(8,128)(2,1)}, u32[]{:S(2)}, u32[]{:S(2)}) %all-to-all-start.1) | async-done | bytes 4194336 | tf_op jit(solution)/shard_map/all_to_all | solution.py:211
  921.6 12.7 %unpack2.1 = bf16[4,2048,768]{2,1,0:T(8,128)(2,1)} custom-call(bf16[8,2048,128]{2,1,0:T(8,128)(2,1)} %all-to-all-done.1.src, bf16[4,2048,768]{2,1,0:T(8,128)(2,1)} %unpack1.1.refs_0_), custom_call_target="tpu_custom_call", output_to_operand_aliasing={{}: (1, {})} | custom-call | flops 50000000 | bytes 8388608 | tf_op jit(solution)/shard_map/unpack2/pallas_call | solution.py:171
  (1 shorter events, 0.0 us)
Async XLA Ops:
  32.7 99.0 %all-to-all-start.4 = ((bf16[8,2048,128]{2,1,0:T(8,128)(2,1)}), bf16[8,2048,128]{2,1,0:T(8,128)(2,1)}, u32[]{:S(2)}, u32[]{:S(2)}) async-start(bf16[8,2048,128]{2,1,0:T(8,128)(2,1)} %pack0.1), calls=%async_computation.4 | async-start | bytes 8388608 | tf_op jit(solution)/shard_map/all_to_all | solution.py:209
  131.7 98.3 %all-to-all-start.2 = ((bf16[8,2048,128]{2,1,0:T(8,128)(2,1)}), bf16[8,2048,128]{2,1,0:T(8,128)(2,1)}, u32[]{:S(2)}, u32[]{:S(2)}) async-start(bf16[8,2048,128]{2,1,0:T(8,128)(2,1)} %pack1.1), calls=%async_computation.2 | async-start | bytes 8388608 | tf_op jit(solution)/shard_map/all_to_all | solution.py:209
  229.9 197.2 %all-to-all-start = ((bf16[8,2048,128]{2,1,0:T(8,128)(2,1)}), bf16[8,2048,128]{2,1,0:T(8,128)(2,1)}, u32[]{:S(2)}, u32[]{:S(2)}) async-start(bf16[8,2048,128]{2,1,0:T(8,128)(2,1)} %pack2.1), calls=%async_computation | async-start | bytes 8388608 | tf_op jit(solution)/shard_map/all_to_all | solution.py:209
  427.2 197.7 %all-to-all-start.5 = ((bf16[8,2048,128]{2,1,0:T(8,128)(2,1)}), bf16[8,2048,128]{2,1,0:T(8,128)(2,1)}, u32[]{:S(2)}, u32[]{:S(2)}) async-start(bf16[8,2048,128]{2,1,0:T(8,128)(2,1)} %bitcast.23), calls=%async_computation.5 | async-start | bytes 8388608 | tf_op jit(solution)/shard_map/all_to_all | solution.py:211
  624.9 197.8 %all-to-all-start.3 = ((bf16[8,2048,128]{2,1,0:T(8,128)(2,1)}), bf16[8,2048,128]{2,1,0:T(8,128)(2,1)}, u32[]{:S(2)}, u32[]{:S(2)}) async-start(bf16[8,2048,128]{2,1,0:T(8,128)(2,1)} %bitcast.22), calls=%async_computation.3 | async-start | bytes 8388608 | tf_op jit(solution)/shard_map/all_to_all | solution.py:211
  822.7 98.9 %all-to-all-start.1 = ((bf16[8,2048,128]{2,1,0:T(8,128)(2,1)}), bf16[8,2048,128]{2,1,0:T(8,128)(2,1)}, u32[]{:S(2)}, u32[]{:S(2)}) async-start(bf16[8,2048,128]{2,1,0:T(8,128)(2,1)} %bitcast.21), calls=%async_computation.1 | async-start | bytes 8388608 | tf_op jit(solution)/shard_map/all_to_all | solution.py:211

commit v2 on v1

v2 whole, which is shorter than its diff:
```python
import functools

import jax
import jax.numpy as jnp
from jax import lax
from jax.experimental import pallas as pl
from jax.experimental.pallas import tpu as pltpu
from jax.sharding import PartitionSpec as P

LANES = 128
FOLDS = (2, 4)
PACK_STEP = 128
WALK_STEP = 512
SUB = 8
SPAN = 128


def lane_block(shape, fold):
    return lax.broadcasted_iota(jnp.int32, shape, 1) // (LANES // fold)


def swap_blocks(parts):
    fold = len(parts)
    wide = LANES // fold
    block = lane_block(parts[0].shape, fold)
    reach = 1
    while reach < fold:
        upper = (block // reach) % 2 == 1
        out = [None] * fold
        for k in range(fold):
            if (k // reach) % 2 == 0:
                a, b = parts[k], parts[k + reach]
                out[k] = jnp.where(upper, pltpu.roll(b, reach * wide, 1), a)
                out[k + reach] = jnp.where(upper, b, pltpu.roll(a, LANES - reach * wide, 1))
        parts = out
        reach *= 2
    return parts


def pack_kernel(fold, src, dst):
    step_rows = src.shape[1]

    def step(k, carry):
        rows = pl.ds(pl.multiple_of(k * PACK_STEP, PACK_STEP), PACK_STEP)
        for t in range(dst.shape[0] // fold):
            cols = slice(t * LANES, (t + 1) * LANES)
            parts = [src[q, rows, cols].astype(jnp.float32) for q in range(fold)]
            for l, part in enumerate(swap_blocks(parts)):
                dst[t * fold + l, rows, :] = part.astype(jnp.bfloat16)
        return carry

    lax.fori_loop(0, step_rows // PACK_STEP, step, 0)


def unpack_kernel(fold, src, *refs):
    dst = refs[-1]
    step_rows = src.shape[1]

    def step(k, carry):
        rows = pl.ds(pl.multiple_of(k * PACK_STEP, PACK_STEP), PACK_STEP)
        for t in range(src.shape[0] // fold):
            cols = slice(t * LANES, (t + 1) * LANES)
            parts = [src[t * fold + l, rows, :].astype(jnp.float32) for l in range(fold)]
            for q, part in enumerate(swap_blocks(parts)):
                dst[q, rows, cols] = part.astype(jnp.bfloat16)
        return carry

    lax.fori_loop(0, step_rows // PACK_STEP, step, 0)


def walk_kernel(group_size, fold, order, starts, spans, src, dst, grid_rows):
    packed_rows = src.shape[0]
    part = packed_rows // group_size
    step_rows = min(WALK_STEP, part)
    wide = LANES // fold

    def place(k):
        base = pl.multiple_of(k * step_rows, step_rows)
        dev = base // part
        return base, [pl.multiple_of((dev * fold + q) * part + base % part, step_rows) for q in range(fold)]

    def spread(k, carry):
        base, at = place(k)
        data = src[pl.ds(base, step_rows), :].astype(jnp.float32)
        for q in range(fold):
            grid_rows[pl.ds(at[q], step_rows), :] = data if q == 0 else pltpu.roll(data, LANES - q * wide, 1)
        return carry

    lax.fori_loop(0, packed_rows // step_rows, spread, 0)

    def load(base):
        index = [order[base + u] for u in range(SUB)]
        return index, [grid_rows[pl.ds(i, 1), :] for i in index]

    def plain(n, total):
        base = n * SPAN
        index, rows = load(base)
        for k in range(SPAN // SUB):
            now_index, now_rows = index, rows
            if k + 1 < SPAN // SUB:
                index, rows = load(base + (k + 1) * SUB)
            for g in range(0, SUB, 4):
                a, b, c, d = now_rows[g:g + 4]
                ab = a + b
                abc = ab + c
                abcd = ab + (c + d)
                sums = (total + a, total + ab, total + abc, total + abcd)
                total = sums[3]
                for u in range(4):
                    grid_rows[pl.ds(now_index[g + u], 1), :] = sums[u]
        return total

    def broken(n, total):
        def one(u, total):
            t = n * SPAN + u
            row = pl.ds(order[t], 1)
            new = starts[t // 16]
            fresh = ((new >> (t % 16)) & 1) == 1
            value = grid_rows[row, :]
            total = jnp.where(fresh, value, total + value)
            grid_rows[row, :] = total
            return total

        return lax.fori_loop(0, SPAN, one, total)

    def walk(n, total):
        return lax.cond(spans[0, n] == 0, plain, broken, n, total)

    lax.fori_loop(0, spans.shape[1], walk, jnp.zeros((1, LANES), jnp.float32))

    block = lane_block((step_rows, LANES), fold)

    def merge(k, carry):
        base, at = place(k)
        merged = grid_rows[pl.ds(at[0], step_rows), :]
        for q in range(1, fold):
            moved = pltpu.roll(grid_rows[pl.ds(at[q], step_rows), :], q * wide, 1)
            merged = jnp.where(block == q, moved, merged)
        dst[pl.ds(base, step_rows), :] = merged.astype(jnp.bfloat16)
        return carry

    lax.fori_loop(0, packed_rows // step_rows, merge, 0)


def solution(mesh):
    group_size = mesh.shape['group']

    def per_device(sort_keys, seg_ids, payload):
        rows_dev = sort_keys.shape[0]
        width = payload.shape[1]
        count = group_size * rows_dev
        tile = min(512, rows_dev // max(FOLDS))
        cols = [group_size * (LANES // fold) for fold in FOLDS]
        begin = [sum(cols[:c]) for c in range(len(FOLDS))]

        def estimate(c, flops):
            return pl.CostEstimate(flops=flops, bytes_accessed=4 * rows_dev * cols[c], transcendentals=0)

        def pack(c, rows):
            fold = FOLDS[c]
            part = rows_dev // fold
            return pl.pallas_call(
                functools.partial(pack_kernel, fold), name=f'pack{c}',
                out_shape=jax.ShapeDtypeStruct((group_size, part, LANES), jnp.bfloat16),
                grid=(part // tile,),
                in_specs=[pl.BlockSpec((fold, tile, cols[c]), lambda i: (0, i, begin[c] // cols[c]))],
                out_specs=pl.BlockSpec((group_size, tile, LANES), lambda i: (0, i, 0)),
                compiler_params=pltpu.CompilerParams(vmem_limit_bytes=60 * 2**20),
                cost_estimate=estimate(c, 50_000_000),
            )(rows.reshape(fold, part, width))

        def unpack(c, back, out):
            fold = FOLDS[c]
            part = rows_dev // fold
            first = out is None
            return pl.pallas_call(
                functools.partial(unpack_kernel, fold), name=f'unpack{c}',
                out_shape=jax.ShapeDtypeStruct((fold, part, width), jnp.bfloat16),
                grid=(part // tile,),
                in_specs=[pl.BlockSpec((group_size, tile, LANES), lambda i: (0, i, 0))]
                + ([] if first else [pl.BlockSpec(memory_space=pl.ANY)]),
                out_specs=pl.BlockSpec((fold, tile, cols[c]), lambda i: (0, i, begin[c] // cols[c])),
                input_output_aliases={} if first else {1: 0},
                compiler_params=pltpu.CompilerParams(vmem_limit_bytes=60 * 2**20),
                cost_estimate=estimate(c, 50_000_000),
            )(*((back,) if first else (back, out.reshape(fold, part, width)))).reshape(rows_dev, width)

        def walk(c, order, starts, spans, rows):
            fold = FOLDS[c]
            return pl.pallas_call(
                functools.partial(walk_kernel, group_size, fold), name=f'walk{c}',
                out_shape=jax.ShapeDtypeStruct((count // fold, LANES), jnp.bfloat16),
                in_specs=[pl.BlockSpec(memory_space=pltpu.SMEM)] * 3 + [pl.BlockSpec(memory_space=pltpu.VMEM)],
                out_specs=pl.BlockSpec(memory_space=pltpu.VMEM),
                scratch_shapes=[pltpu.VMEM((count, LANES), jnp.float32)],
                compiler_params=pltpu.CompilerParams(vmem_limit_bytes=62 * 2**20),
                cost_estimate=estimate(c, 1_000_000_000),
            )(order, starts, spans, rows)

        halves = jnp.stack([sort_keys, (seg_ids >> 16).astype(jnp.float32), (seg_ids & 0xFFFF).astype(jnp.float32)])
        every = lax.all_gather(halves, 'group')
        every, folded = lax.optimization_barrier((every, payload))
        keys = every[:, 0].reshape(count)
        ids = ((every[:, 1].astype(jnp.int32) << 16) | every[:, 2].astype(jnp.int32)).reshape(count)
        first = pack(0, folded)
        _, ids_sorted, order = lax.sort((keys, ids, jnp.arange(count, dtype=jnp.int32)), num_keys=1)
        new = jnp.concatenate([jnp.ones((1,), jnp.bool_), ids_sorted[1:] != ids_sorted[:-1]]).astype(jnp.int32)
        starts = jnp.sum(new.reshape(count // 16, 16) << jnp.arange(16, dtype=jnp.int32)[None, :], axis=1)
        spans = jnp.max(new.reshape(1, count // SPAN, SPAN), axis=2)
        order, starts, spans, folded = lax.optimization_barrier((order, starts, spans, folded))

        sent = [first] + [pack(c, folded) for c in range(1, len(FOLDS))]
        there = [lax.all_to_all(s, 'group', 0, 0, tiled=True) for s in sent]
        done = [walk(c, order, starts, spans, t.reshape(-1, LANES)) for c, t in enumerate(there)]
        back = [lax.all_to_all(d.reshape(group_size, -1, LANES), 'group', 0, 0, tiled=True) for d in done]
        out = None
        for c, b in enumerate(back):
            out = unpack(c, b, out)
        return out

    row_spec = P(('batch', 'group'))
    mat_spec = P(('batch', 'group'), None)
    return jax.shard_map(per_device, mesh=mesh, in_specs=(row_spec, row_spec, mat_spec),
                         out_specs=mat_spec, check_vma=False)
```

time: 935 us -> 649 us (0.69)
  Pallas kernels: 654 us -> 291 us
  waiting for transfers between devices: 173 us -> 260 us
  starting transfers between devices: 29.5 us -> 19.4 us
    pallas_call x9 -> x6, Pallas kernels: 654 us -> 291 us  [the longest x2 254 us: walk(): pl.pallas_call(functools.partial(walk_kernel, group_size, fold), name=f'w...]
    all_to_all x3 -> x2, waiting for transfers between devices: 68.4 us -> 141 us  [per_device(): lax.all_to_all(d.reshape(group_size, -1, LANES), 'group', 0, 0, tiled=True)]
    all_to_all x3 -> x2, waiting for transfers between devices: 105 us -> 119 us  [per_device(): there = [lax.all_to_all(s, 'group', 0, 0, tiled=True) for s in sent]]
  transfers between devices with their start and end apart: 6 -> 4, of which waited for: 3 -> 3; matrix products, arithmetic and copies ran while one was open for 6% -> 9% of each run, Pallas kernels for 67% -> 42%
where the time goes in v2:
time: 649 us; the launch traced here: 648 us
  Pallas kernels  291 us (45%)
  waiting for transfers between devices  260 us (40%)
  other arithmetic  58.1 us (9%)
  starting transfers between devices  19.4 us (3%)
  blocking collectives  18.4 us (3%)
    pallas_call x2, Pallas kernels, walk(): pl.pallas_call(functools.partial(walk_kernel, group_size, fold), name=f'w...  254 us
    all_to_all x2, waiting for transfers between devices, per_device(): lax.all_to_all(d.reshape(group_size, -1, LANES), 'group', 0, 0, tiled=True)  141 us
    all_to_all x2, waiting for transfers between devices, per_device(): there = [lax.all_to_all(s, 'group', 0, 0, tiled=True) for s in sent]  119 us
    sort x1, other arithmetic, per_device(): lax.sort((keys, ids, jnp.arange(count, dtype=jnp.int32)), num_keys=1)  53.5 us
    pallas_call x2, Pallas kernels, pack(): pl.pallas_call(functools.partial(pack_kernel, fold), name=f'pack{c}', out...  18.6 us
    pallas_call x2, Pallas kernels, unpack(): pl.pallas_call(functools.partial(unpack_kernel, fold), name=f'unpack{c}',...  18.4 us
    all_gather x1, blocking collectives, per_device(): every = lax.all_gather(halves, 'group')  18.4 us
  transfers between devices with their start and end apart: 4, of which 3 were waited for; matrix products, arithmetic and copies ran while one was open for 9% of the time, Pallas kernels for 42%

profile of v2, /device:TPU:0, one launch (start us, length us, event | category | flops | bytes accessed | tf_op | source)
XLA Modules:
  0.0 648.0 jit_solution(14249758955738668860)
XLA Ops:
  0.0 0.8 shift-right-arithmetic_convert_fusion
  0.8 0.8 maximum_bitcast_fusion
  1.6 18.4 %all-gather.1 = f32[8,3,8192]{2,1,0:T(4,128)S(1)} all-gather(f32[1,3,8192]{2,1,0:T(4,128)S(1)} %maximum_bitcast_fusion), channel_id=2, replica_groups=mesh['batch'=4,'group'=8] {'group'}, dimensions={0}, use_global_device_ids=true | all-gather | bytes 884736 | tf_op jit(solution)/shard_map/all_gather | solution.py:201
  20.0 10.9 %pack0.1 = bf16[8,4096,128]{2,1,0:T(8,128)(2,1)} custom-call(bf16[2,4096,768]{2,1,0:T(8,128)(2,1)} %bitcast.19), custom_call_target="tpu_custom_call" | custom-call | flops 50000000 | bytes 16777216 | tf_op jit(solution)/shard_map/pack0/pallas_call | solution.py:162
  30.8 5.2 all-to-all-start.2
  36.0 0.2 slice.15
  36.2 0.7 convert_or_fusion
  36.9 53.5 %sort.21 = (f32[65536]{0:T(1024)}, s32[65536]{0:T(1024)S(1)}, s32[65536]{0:T(1024)}) sort(f32[65536]{0:T(1024)S(1)} %bitcast.24, s32[65536]{0:T(1024)S(1)} %bitcast.23, s32[65536]{0:T(1024)S(1)} %iota.7), dimensions={0}, to_apply=%region_0.0 | sort | flops 1048576 | bytes 1572864 | tf_op jit(solution)/shard_map/sort | solution.py:206
  90.4 0.1 slice_compare_fusion
  90.6 0.1 add_convert_fusion
  90.7 0.6 reshape.55
  91.3 0.8 bitcast_reduce_fusion
  92.1 1.2 shift-left_reduce_fusion.starts
  93.3 7.7 %pack1.1 = bf16[8,2048,128]{2,1,0:T(8,128)(2,1)} custom-call(bf16[4,2048,768]{2,1,0:T(8,128)(2,1)} %bitcast.20), custom_call_target="tpu_custom_call" | custom-call | flops 50000000 | bytes 8388608 | tf_op jit(solution)/shard_map/pack1/pallas_call | solution.py:162
  101.1 118.6 %all-to-all-done.2 = bf16[8,4096,128]{2,1,0:T(8,128)(2,1)} async-done(((bf16[8,4096,128]{2,1,0:T(8,128)(2,1)}), bf16[8,4096,128]{2,1,0:T(8,128)(2,1)}, u32[]{:S(2)}, u32[]{:S(2)}) %all-to-all-start.2) | async-done | bytes 8388640 | tf_op jit(solution)/shard_map/all_to_all | solution.py:213
  219.7 4.6 all-to-all-start
  224.3 129.1 %walk0.1 = bf16[32768,128]{1,0:T(8,128)(2,1)} custom-call(s32[65536]{0:T(1024)} %get-tuple-element.17.order, s32[4096]{0:T(1024)} %shift-left_reduce_fusion.starts, s32[1,512]{1,0:T(1,128)} %bitcast.28, bf16[32768,128]{1,0:T(8,128)(2,1)} %bitcast.12.src), custom_call_target="tpu_custom_call" | custom-call | flops 1000000000 | bytes 16777216 | tf_op jit(solution)/shard_map/walk0/pallas_call | solution.py:190
  353.4 0.0 all-to-all-done
  353.4 5.0 all-to-all-start.3
  358.4 125.2 %walk1.1 = bf16[16384,128]{1,0:T(8,128)(2,1)} custom-call(s32[65536]{0:T(1024)} %get-tuple-element.17.order, s32[4096]{0:T(1024)} %shift-left_reduce_fusion.starts, s32[1,512]{1,0:T(1,128)} %bitcast.29, bf16[16384,128]{1,0:T(8,128)(2,1)} %bitcast.9.src), custom_call_target="tpu_custom_call" | custom-call | flops 1000000000 | bytes 8388608 | tf_op jit(solution)/shard_map/walk1/pallas_call | solution.py:190
  483.6 58.5 %all-to-all-done.3.src = bf16[8,4096,128]{2,1,0:T(8,128)(2,1)} async-done(((bf16[8,4096,128]{2,1,0:T(8,128)(2,1)}), bf16[8,4096,128]{2,1,0:T(8,128)(2,1)}, u32[]{:S(2)}, u32[]{:S(2)}) %all-to-all-start.3) | async-done | bytes 8388640 | tf_op jit(solution)/shard_map/all_to_all | solution.py:215
  542.0 4.6 all-to-all-start.1
  546.7 10.7 %unpack0.1 = bf16[2,4096,768]{2,1,0:T(8,128)(2,1)} custom-call(bf16[8,4096,128]{2,1,0:T(8,128)(2,1)} %all-to-all-done.3.src), custom_call_target="tpu_custom_call" | custom-call | flops 50000000 | bytes 16777216 | tf_op jit(solution)/shard_map/unpack0/pallas_call | solution.py:176
  557.4 82.9 %all-to-all-done.1.src = bf16[8,2048,128]{2,1,0:T(8,128)(2,1)} async-done(((bf16[8,2048,128]{2,1,0:T(8,128)(2,1)}), bf16[8,2048,128]{2,1,0:T(8,128)(2,1)}, u32[]{:S(2)}, u32[]{:S(2)}) %all-to-all-start.1) | async-done | bytes 4194336 | tf_op jit(solution)/shard_map/all_to_all | solution.py:215
  640.3 7.6 %unpack1.1 = bf16[4,2048,768]{2,1,0:T(8,128)(2,1)} custom-call(bf16[8,2048,128]{2,1,0:T(8,128)(2,1)} %all-to-all-done.1.src, bf16[4,2048,768]{2,1,0:T(8,128)(2,1)} %bitcast.18), custom_call_target="tpu_custom_call", output_to_operand_aliasing={{}: (1, {})} | custom-call | flops 50000000 | bytes 8388608 | tf_op jit(solution)/shard_map/unpack1/pallas_call | solution.py:176
  (1 shorter events, 0.0 us)
Async XLA Ops:
  30.8 188.8 %all-to-all-start.2 = ((bf16[8,4096,128]{2,1,0:T(8,128)(2,1)}), bf16[8,4096,128]{2,1,0:T(8,128)(2,1)}, u32[]{:S(2)}, u32[]{:S(2)}) async-start(bf16[8,4096,128]{2,1,0:T(8,128)(2,1)} %pack0.1), calls=%async_computation.2 | async-start | bytes 16777216 | tf_op jit(solution)/shard_map/all_to_all | solution.py:213
  219.7 133.7 %all-to-all-start = ((bf16[8,2048,128]{2,1,0:T(8,128)(2,1)}), bf16[8,2048,128]{2,1,0:T(8,128)(2,1)}, u32[]{:S(2)}, u32[]{:S(2)}) async-start(bf16[8,2048,128]{2,1,0:T(8,128)(2,1)} %pack1.1), calls=%async_computation | async-start | bytes 8388608 | tf_op jit(solution)/shard_map/all_to_all | solution.py:213
  353.4 188.7 %all-to-all-start.3 = ((bf16[8,4096,128]{2,1,0:T(8,128)(2,1)}), bf16[8,4096,128]{2,1,0:T(8,128)(2,1)}, u32[]{:S(2)}, u32[]{:S(2)}) async-start(bf16[8,4096,128]{2,1,0:T(8,128)(2,1)} %bitcast.21), calls=%async_computation.3 | async-start | bytes 16777216 | tf_op jit(solution)/shard_map/all_to_all | solution.py:215
  542.0 98.3 %all-to-all-start.1 = ((bf16[8,2048,128]{2,1,0:T(8,128)(2,1)}), bf16[8,2048,128]{2,1,0:T(8,128)(2,1)}, u32[]{:S(2)}, u32[]{:S(2)}) async-start(bf16[8,2048,128]{2,1,0:T(8,128)(2,1)} %bitcast.22), calls=%async_computation.1 | async-start | bytes 8388608 | tf_op jit(solution)/shard_map/all_to_all | solution.py:215

commit v3 on v2

--- a/solution.py
+++ b/solution.py
@@ -13,6 +13,7 @@
 WALK_STEP = 512
 SUB = 8
 SPAN = 128
+BITS = 16
 
 
 def lane_block(shape, fold):
@@ -68,37 +69,61 @@
     lax.fori_loop(0, step_rows // PACK_STEP, step, 0)
 
 
-def walk_kernel(group_size, fold, order, starts, spans, src, dst, grid_rows):
-    packed_rows = src.shape[0]
+def walk_kernel(group_size, fold, order_hbm, starts, spans, src, dst, grid_rows, stage, order, in_sem, out_sem, order_sem):
+    packed_rows = stage.shape[0]
     part = packed_rows // group_size
     step_rows = min(WALK_STEP, part)
     wide = LANES // fold
-
-    def place(k):
-        base = pl.multiple_of(k * step_rows, step_rows)
-        dev = base // part
-        return base, [pl.multiple_of((dev * fold + q) * part + base % part, step_rows) for q in range(fold)]
-
-    def spread(k, carry):
-        base, at = place(k)
-        data = src[pl.ds(base, step_rows), :].astype(jnp.float32)
-        for q in range(fold):
-            grid_rows[pl.ds(at[q], step_rows), :] = data if q == 0 else pltpu.roll(data, LANES - q * wide, 1)
-        return carry
-
-    lax.fori_loop(0, packed_rows // step_rows, spread, 0)
-
-    def load(base):
-        index = [order[base + u] for u in range(SUB)]
+    piece = order.shape[0] // group_size
+    piece_spans = piece // SPAN
+
+    def part_rows(d):
+        return pl.ds(pl.multiple_of(d * part, part), part)
+
+    def copy_in(d):
+        return pltpu.make_async_copy(src.at[part_rows(d)], stage.at[part_rows(d)], in_sem.at[d])
+
+    def copy_out(d):
+        return pltpu.make_async_copy(stage.at[part_rows(d)], dst.at[part_rows(d)], out_sem.at[d])
+
+    def copy_order(d):
+        rows = pl.ds(pl.multiple_of(d * piece, piece), piece)
+        return pltpu.make_async_copy(order_hbm.at[rows], order.at[rows], order_sem.at[d])
+
+    for d in range(group_size):
+        copy_in(d).start()
+    for d in range(group_size):
+        copy_order(d).start()
+
+    def place(d, k):
+        base = pl.multiple_of(d * part + k * step_rows, step_rows)
+        return base, [pl.multiple_of((d * fold + q) * part + k * step_rows, step_rows) for q in range(fold)]
+
+    def spread(d, carry):
+        copy_in(d).wait()
+
+        def step(k, carry):
+            base, at = place(d, k)
+            data = stage[pl.ds(base, step_rows), :].astype(jnp.float32)
+            for q in range(fold):
+                grid_rows[pl.ds(at[q], step_rows), :] = data if q == 0 else pltpu.roll(data, LANES - q * wide, 1)
+            return carry
+
+        return lax.fori_loop(0, part // step_rows, step, carry)
+
+    lax.fori_loop(0, group_size, spread, 0)
+
+    def load(base, rows):
+        index = [order[base + u] for u in range(rows)]
         return index, [grid_rows[pl.ds(i, 1), :] for i in index]
 
     def plain(n, total):
         base = n * SPAN
-        index, rows = load(base)
+        index, rows = load(base, SUB)
         for k in range(SPAN // SUB):
             now_index, now_rows = index, rows
             if k + 1 < SPAN // SUB:
-                index, rows = load(base + (k + 1) * SUB)
+                index, rows = load(base + (k + 1) * SUB, SUB)
             for g in range(0, SUB, 4):
                 a, b, c, d = now_rows[g:g + 4]
                 ab = a + b
@@ -111,35 +136,48 @@
         return total
 
     def broken(n, total):
-        def one(u, total):
-            t = n * SPAN + u
-            row = pl.ds(order[t], 1)
-            new = starts[t // 16]
-            fresh = ((new >> (t % 16)) & 1) == 1
-            value = grid_rows[row, :]
-            total = jnp.where(fresh, value, total + value)
-            grid_rows[row, :] = total
+        def sixteen(j, total):
+            group = n * (SPAN // BITS) + j
+            bits = starts[group]
+            index, rows = load(group * BITS, BITS)
+            for u in range(BITS):
+                total = jnp.where(((bits >> u) & 1) == 1, rows[u], total + rows[u])
+                rows[u] = total
+            for u in range(BITS):
+                grid_rows[pl.ds(index[u], 1), :] = rows[u]
             return total
 
-        return lax.fori_loop(0, SPAN, one, total)
-
-    def walk(n, total):
-        return lax.cond(spans[0, n] == 0, plain, broken, n, total)
-
-    lax.fori_loop(0, spans.shape[1], walk, jnp.zeros((1, LANES), jnp.float32))
+        return lax.fori_loop(0, SPAN // BITS, sixteen, total)
+
+    def walk(d, total):
+        copy_order(d).wait()
+
+        def span(n, total):
+            return lax.cond(spans[0, n] == 0, plain, broken, n, total)
+
+        return lax.fori_loop(d * piece_spans, (d + 1) * piece_spans, span, total)
+
+    lax.fori_loop(0, group_size, walk, jnp.zeros((1, LANES), jnp.float32))
 
     block = lane_block((step_rows, LANES), fold)
 
-    def merge(k, carry):
-        base, at = place(k)
-        merged = grid_rows[pl.ds(at[0], step_rows), :]
-        for q in range(1, fold):
-            moved = pltpu.roll(grid_rows[pl.ds(at[q], step_rows), :], q * wide, 1)
-            merged = jnp.where(block == q, moved, merged)
-        dst[pl.ds(base, step_rows), :] = merged.astype(jnp.bfloat16)
+    def merge(d, carry):
+        def step(k, carry):
+            base, at = place(d, k)
+            merged = grid_rows[pl.ds(at[0], step_rows), :]
+            for q in range(1, fold):
+                moved = pltpu.roll(grid_rows[pl.ds(at[q], step_rows), :], q * wide, 1)
+                merged = jnp.where(block == q, moved, merged)
+            stage[pl.ds(base, step_rows), :] = merged.astype(jnp.bfloat16)
+            return carry
+
+        carry = lax.fori_loop(0, part // step_rows, step, carry)
+        copy_out(d).start()
         return carry
 
-    lax.fori_loop(0, packed_rows // step_rows, merge, 0)
+    lax.fori_loop(0, group_size, merge, 0)
+    for d in range(group_size):
+        copy_out(d).wait()
 
 
 def solution(mesh):
@@ -190,9 +228,17 @@
             return pl.pallas_call(
                 functools.partial(walk_kernel, group_size, fold), name=f'walk{c}',
                 out_shape=jax.ShapeDtypeStruct((count // fold, LANES), jnp.bfloat16),
-                in_specs=[pl.BlockSpec(memory_space=pltpu.SMEM)] * 3 + [pl.BlockSpec(memory_space=pltpu.VMEM)],
-                out_specs=pl.BlockSpec(memory_space=pltpu.VMEM),
-                scratch_shapes=[pltpu.VMEM((count, LANES), jnp.float32)],
+                in_specs=[pl.BlockSpec(memory_space=pl.ANY)] + [pl.BlockSpec(memory_space=pltpu.SMEM)] * 2
+                + [pl.BlockSpec(memory_space=pl.ANY)],
+                out_specs=pl.BlockSpec(memory_space=pl.ANY),
+                scratch_shapes=[
+                    pltpu.VMEM((count, LANES), jnp.float32),
+                    pltpu.VMEM((count // fold, LANES), jnp.bfloat16),
+                    pltpu.SMEM((count,), jnp.int32),
+                    pltpu.SemaphoreType.DMA((group_size,)),
+                    pltpu.SemaphoreType.DMA((group_size,)),
+                    pltpu.SemaphoreType.DMA((group_size,)),
+                ],
                 compiler_params=pltpu.CompilerParams(vmem_limit_bytes=62 * 2**20),
                 cost_estimate=estimate(c, 1_000_000_000),
             )(order, starts, spans, rows)
@@ -205,7 +251,7 @@
         first = pack(0, folded)
         _, ids_sorted, order = lax.sort((keys, ids, jnp.arange(count, dtype=jnp.int32)), num_keys=1)
         new = jnp.concatenate([jnp.ones((1,), jnp.bool_), ids_sorted[1:] != ids_sorted[:-1]]).astype(jnp.int32)
-        starts = jnp.sum(new.reshape(count // 16, 16) << jnp.arange(16, dtype=jnp.int32)[None, :], axis=1)
+        starts = jnp.sum(new.reshape(count // BITS, BITS) << jnp.arange(BITS, dtype=jnp.int32)[None, :], axis=1)
         spans = jnp.max(new.reshape(1, count // SPAN, SPAN), axis=2)
         order, starts, spans, folded = lax.optimization_barrier((order, starts, spans, folded))
 

time: 649 us -> 629 us (0.969)
  Pallas kernels: 291 us -> 252 us
  waiting for transfers between devices: 260 us -> 279 us
    pallas_call x2, Pallas kernels: 254 us -> 215 us  [walk(): pl.pallas_call(functools.partial(walk_kernel, group_size, fold), name=f'w...]
    all_to_all x2, waiting for transfers between devices: 141 us -> 161 us  [per_device(): lax.all_to_all(d.reshape(group_size, -1, LANES), 'group', 0, 0, tiled=True)]
  transfers between devices with their start and end apart: 4 -> 4, of which waited for: 3 -> 3; matrix products, arithmetic and copies ran while one was open for 9% -> 9% of each run, Pallas kernels for 42% -> 37%
where the time goes in v3:
time: 629 us; the launch traced here: 628 us
  waiting for transfers between devices  279 us (44%)
  Pallas kernels  252 us (40%)
  other arithmetic  58.1 us (9%)
  starting transfers between devices  19.4 us (3%)
  blocking collectives  18.4 us (3%)
    pallas_call x2, Pallas kernels, walk(): pl.pallas_call(functools.partial(walk_kernel, group_size, fold), name=f'w...  215 us
    all_to_all x2, waiting for transfers between devices, per_device(): lax.all_to_all(d.reshape(group_size, -1, LANES), 'group', 0, 0, tiled=True)  161 us
    all_to_all x2, waiting for transfers between devices, per_device(): there = [lax.all_to_all(s, 'group', 0, 0, tiled=True) for s in sent]  119 us
    sort x1, other arithmetic, per_device(): lax.sort((keys, ids, jnp.arange(count, dtype=jnp.int32)), num_keys=1)  53.5 us
    pallas_call x2, Pallas kernels, pack(): pl.pallas_call(functools.partial(pack_kernel, fold), name=f'pack{c}', out...  18.6 us
    pallas_call x2, Pallas kernels, unpack(): pl.pallas_call(functools.partial(unpack_kernel, fold), name=f'unpack{c}',...  18.4 us
    all_gather x1, blocking collectives, per_device(): every = lax.all_gather(halves, 'group')  18.4 us
  transfers between devices with their start and end apart: 4, of which 3 were waited for; matrix products, arithmetic and copies ran while one was open for 9% of the time, Pallas kernels for 37%

profile of v3, /device:TPU:0, one launch (start us, length us, event | category | flops | bytes accessed | tf_op | source)
XLA Modules:
  0.0 627.6 jit_solution(16022529109177528684)
XLA Ops:
  0.0 0.8 shift-right-arithmetic_convert_fusion
  0.8 0.8 maximum_bitcast_fusion
  1.6 18.4 %all-gather.1 = f32[8,3,8192]{2,1,0:T(4,128)S(1)} all-gather(f32[1,3,8192]{2,1,0:T(4,128)S(1)} %maximum_bitcast_fusion), channel_id=2, replica_groups=mesh['batch'=4,'group'=8] {'group'}, dimensions={0}, use_global_device_ids=true | all-gather | bytes 884736 | tf_op jit(solution)/shard_map/all_gather | solution.py:247
  20.0 10.9 %pack0.1 = bf16[8,4096,128]{2,1,0:T(8,128)(2,1)} custom-call(bf16[2,4096,768]{2,1,0:T(8,128)(2,1)} %bitcast.19), custom_call_target="tpu_custom_call" | custom-call | flops 50000000 | bytes 16777216 | tf_op jit(solution)/shard_map/pack0/pallas_call | solution.py:200
  30.8 5.2 all-to-all-start.2
  36.0 0.2 slice.15
  36.2 0.7 convert_or_fusion
  36.9 53.5 %sort.21 = (f32[65536]{0:T(1024)}, s32[65536]{0:T(1024)S(1)}, s32[65536]{0:T(1024)}) sort(f32[65536]{0:T(1024)S(1)} %bitcast.24, s32[65536]{0:T(1024)S(1)} %bitcast.23, s32[65536]{0:T(1024)S(1)} %iota.7), dimensions={0}, to_apply=%region_0.0 | sort | flops 1048576 | bytes 1572864 | tf_op jit(solution)/shard_map/sort | solution.py:252
  90.4 0.1 slice_compare_fusion
  90.6 0.1 add_convert_fusion
  90.7 0.6 reshape.55
  91.3 0.8 bitcast_reduce_fusion
  92.1 1.2 shift-left_reduce_fusion.starts
  93.3 7.7 %pack1.1 = bf16[8,2048,128]{2,1,0:T(8,128)(2,1)} custom-call(bf16[4,2048,768]{2,1,0:T(8,128)(2,1)} %bitcast.20), custom_call_target="tpu_custom_call" | custom-call | flops 50000000 | bytes 8388608 | tf_op jit(solution)/shard_map/pack1/pallas_call | solution.py:200
  101.1 118.6 %all-to-all-done.2 = bf16[8,4096,128]{2,1,0:T(8,128)(2,1)} async-done(((bf16[8,4096,128]{2,1,0:T(8,128)(2,1)}), bf16[8,4096,128]{2,1,0:T(8,128)(2,1)}, u32[]{:S(2)}, u32[]{:S(2)}) %all-to-all-start.2) | async-done | bytes 8388640 | tf_op jit(solution)/shard_map/all_to_all | solution.py:259
  219.7 4.6 all-to-all-start
  224.3 108.7 %walk0.1 = bf16[32768,128]{1,0:T(8,128)(2,1)} custom-call(s32[65536]{0:T(1024)} %get-tuple-element.17.order_hbm, s32[4096]{0:T(1024)} %shift-left_reduce_fusion.starts, s32[1,512]{1,0:T(1,128)} %bitcast.28, bf16[32768,128]{1,0:T(8,128)(2,1)} %bitcast.12.src), custom_call_target="tpu_custom_call" | custom-call | flops 1000000000 | bytes 16777216 | tf_op jit(solution)/shard_map/walk0/pallas_call | solution.py:228
  333.0 0.0 all-to-all-done
  333.0 5.0 all-to-all-start.3
  338.0 106.0 %walk1.1 = bf16[16384,128]{1,0:T(8,128)(2,1)} custom-call(s32[65536]{0:T(1024)} %get-tuple-element.17.order_hbm, s32[4096]{0:T(1024)} %shift-left_reduce_fusion.starts, s32[1,512]{1,0:T(1,128)} %bitcast.29, bf16[16384,128]{1,0:T(8,128)(2,1)} %bitcast.9.src), custom_call_target="tpu_custom_call" | custom-call | flops 1000000000 | bytes 8388608 | tf_op jit(solution)/shard_map/walk1/pallas_call | solution.py:228
  444.0 77.6 %all-to-all-done.3.src = bf16[8,4096,128]{2,1,0:T(8,128)(2,1)} async-done(((bf16[8,4096,128]{2,1,0:T(8,128)(2,1)}), bf16[8,4096,128]{2,1,0:T(8,128)(2,1)}, u32[]{:S(2)}, u32[]{:S(2)}) %all-to-all-start.3) | async-done | bytes 8388640 | tf_op jit(solution)/shard_map/all_to_all | solution.py:261
  521.7 4.6 all-to-all-start.1
  526.3 10.7 %unpack0.1 = bf16[2,4096,768]{2,1,0:T(8,128)(2,1)} custom-call(bf16[8,4096,128]{2,1,0:T(8,128)(2,1)} %all-to-all-done.3.src), custom_call_target="tpu_custom_call" | custom-call | flops 50000000 | bytes 16777216 | tf_op jit(solution)/shard_map/unpack0/pallas_call | solution.py:214
  537.0 82.9 %all-to-all-done.1.src = bf16[8,2048,128]{2,1,0:T(8,128)(2,1)} async-done(((bf16[8,2048,128]{2,1,0:T(8,128)(2,1)}), bf16[8,2048,128]{2,1,0:T(8,128)(2,1)}, u32[]{:S(2)}, u32[]{:S(2)}) %all-to-all-start.1) | async-done | bytes 4194336 | tf_op jit(solution)/shard_map/all_to_all | solution.py:261
  620.0 7.6 %unpack1.1 = bf16[4,2048,768]{2,1,0:T(8,128)(2,1)} custom-call(bf16[8,2048,128]{2,1,0:T(8,128)(2,1)} %all-to-all-done.1.src, bf16[4,2048,768]{2,1,0:T(8,128)(2,1)} %bitcast.18), custom_call_target="tpu_custom_call", output_to_operand_aliasing={{}: (1, {})} | custom-call | flops 50000000 | bytes 8388608 | tf_op jit(solution)/shard_map/unpack1/pallas_call | solution.py:214
  (1 shorter events, 0.0 us)
Async XLA Ops:
  30.8 188.8 %all-to-all-start.2 = ((bf16[8,4096,128]{2,1,0:T(8,128)(2,1)}), bf16[8,4096,128]{2,1,0:T(8,128)(2,1)}, u32[]{:S(2)}, u32[]{:S(2)}) async-start(bf16[8,4096,128]{2,1,0:T(8,128)(2,1)} %pack0.1), calls=%async_computation.2 | async-start | bytes 16777216 | tf_op jit(solution)/shard_map/all_to_all | solution.py:259
  219.7 113.3 %all-to-all-start = ((bf16[8,2048,128]{2,1,0:T(8,128)(2,1)}), bf16[8,2048,128]{2,1,0:T(8,128)(2,1)}, u32[]{:S(2)}, u32[]{:S(2)}) async-start(bf16[8,2048,128]{2,1,0:T(8,128)(2,1)} %pack1.1), calls=%async_computation | async-start | bytes 8388608 | tf_op jit(solution)/shard_map/all_to_all | solution.py:259
  333.0 188.7 %all-to-all-start.3 = ((bf16[8,4096,128]{2,1,0:T(8,128)(2,1)}), bf16[8,4096,128]{2,1,0:T(8,128)(2,1)}, u32[]{:S(2)}, u32[]{:S(2)}) async-start(bf16[8,4096,128]{2,1,0:T(8,128)(2,1)} %bitcast.21), calls=%async_computation.3 | async-start | bytes 16777216 | tf_op jit(solution)/shard_map/all_to_all | solution.py:261
  521.7 98.3 %all-to-all-start.1 = ((bf16[8,2048,128]{2,1,0:T(8,128)(2,1)}), bf16[8,2048,128]{2,1,0:T(8,128)(2,1)}, u32[]{:S(2)}, u32[]{:S(2)}) async-start(bf16[8,2048,128]{2,1,0:T(8,128)(2,1)} %bitcast.22), calls=%async_computation.1 | async-start | bytes 8388608 | tf_op jit(solution)/shard_map/all_to_all | solution.py:261
